TPU v7x, 32 devices: a whole 2x2x4 slice. The times are simulated.
32 devices in a mesh: replica: 4 (over x, core), fsdp: 8 (over z, y).
Axes of the slice: x: 2, y: 2, z: 4, core: 2. Of those that a mesh axis runs over, the one named last changes fastest.
Arguments:
- deltas: bfloat16 [4, 2, 2048, 16384], P('replica', None, 'fsdp'), may hold values from -3 to 3
- master: float32 [2, 2048, 16384], P(None, 'replica', 'fsdp'), may hold values from -3 to 3
- momentum: float32 [2, 2048, 16384], P(None, 'replica', 'fsdp'), may hold values from -2 to 2
Outputs:
- master_out: float32 [2, 2048, 16384], P(None, 'replica', 'fsdp')
- momentum_out: float32 [2, 2048, 16384], P(None, 'replica', 'fsdp')
- params_out: bfloat16 [2, 2048, 16384], P(None, 'fsdp')
All inputs are finite; a program needn't handle non-finite values.
Results may differ from a plain program's by a relative error of at most 0.008.
Values may be sent and summed in bfloat16 or wider, within the bound.
A program may use at most 128 MiB of HBM per device.

v0:
```python
import jax
import jax.numpy as jnp
from jax import lax
from jax.sharding import PartitionSpec as P


def on_device(deltas, master, momentum):
    local = deltas[0]
    groups = lax.axis_size("replica")
    moved = lax.all_to_all(local, "fsdp", split_axis=2, concat_axis=1, tiled=True)
    summed = lax.psum_scatter(
        moved.astype(jnp.float32).astype(jnp.bfloat16), "replica", scatter_dimension=1, tiled=True
    ).astype(jnp.float32)
    outer = summed / groups
    velocity = 0.9 * momentum + outer
    updated = master - 0.7 * (outer + 0.9 * velocity)
    rounded = updated.astype(jnp.bfloat16)
    copies = lax.all_gather(rounded, "replica", axis=1, tiled=True)
    spread = lax.all_to_all(copies, "fsdp", split_axis=1, concat_axis=2, tiled=True)
    return (updated, velocity, spread)


def solution(mesh):
    return jax.shard_map(
        on_device,
        mesh=mesh,
        in_specs=(
            P("replica", None, "fsdp", None),
            P(None, "replica", "fsdp"),
            P(None, "replica", "fsdp"),
        ),
        out_specs=(P(None, "replica", "fsdp"), P(None, "replica", "fsdp"), P(None, "fsdp", None)),
        check_vma=False,
    )
```

profile of v0, /device:TPU:0, one launch (start us, length us, event | category | flops | bytes accessed | tf_op | source)
XLA Modules:
  0.0 1325.4 jit_solution(8873194051052167290)
XLA Ops:
  7.2 0.0 all-reduce.3.cloned.1.call-start
  7.2 40.8 %copy.22 = bf16[1,2,256,16384]{2,1,3,0:T(2,128)(2,1)} copy(bf16[1,2,256,16384]{3,2,1,0:T(8,128)(2,1)} %param.3) | data formatting | bytes 33554432 | tf_op args[0]
  48.0 372.0 %all_to_all.36 = bf16[2,256,16384]{1,0,2:T(2,128)(2,1)} all-to-all(bf16[2,256,16384]{1,0,2:T(2,128)(2,1)} %bitcast.14), channel_id=1, replica_groups=mesh['replica'=4,'fsdp'=8] {'fsdp'}, dimensions={2} | all-to-all | bytes 33554432 | tf_op jit(solution)/shard_map/all_to_all | solution.py:10
  420.0 60.3 %copy.23 = bf16[2,8,256,2048]{3,0,2,1:T(2,128)(2,1)} copy(bf16[2,8,256,2048]{2,0,3,1:T(2,128)(2,1)} %bitcast.12) | data formatting | bytes 33554432 | tf_op jit(solution)/shard_map/all_to_all | solution.py:10
  480.3 0.0 copy-start
  480.3 0.0 all-reduce.3.cloned.1.call-update
  480.3 0.0 all-gather.2.cloned.1.call-start
  480.4 0.6 copy-done
  481.0 0.6 dynamic-slice
  482.2 285.7 %all-reduce.3.cloned.1.call-done = bf16[2,2048,2048]{2,0,1:T(2,128)(2,1)} async-done(((bf16[2,2048,2048]{2,0,1:T(2,128)(2,1)}), bf16[2,2048,2048]{2,0,1:T(2,128)(2,1)}) %all-reduce.3.cloned.1.call-update) | async-done | bytes 16777232
  767.9 5.1 constant_dynamic-slice_fusion
  773.0 13.9 %fusion = (bf16[2,512,2048]{2,1,0:T(8,128)(2,1)}, f32[2,512,2048]{2,1,0:T(8,128)}, f32[2,512,2048]{2,1,0:T(8,128)}) fusion(f32[2,512,2048]{2,1,0:T(8,128)} %param.4, bf16[2,512,2048]{2,0,1:T(2,128)(2,1)S(1)} %constant_dynamic-slice_fusion, f32[2,512,2048]{2,1,0:T(8,128)} %param.5), kind=kLoop, calls=%fused_computation.4 | loop fusion | flops 18874368 | bytes 41943040 | tf_op jit(solution)/shard_map/convert_element_type | solution.py:17
  786.9 8.4 copy.25
  795.3 0.0 all-gather.2.cloned.1.call-update
  795.3 106.1 %all-gather.2.cloned.1.call-done = bf16[2,2048,2048]{2,0,1:T(2,128)(2,1)} async-done(((bf16[2,512,2048]{2,0,1:T(2,128)(2,1)}), bf16[2,2048,2048]{2,0,1:T(2,128)(2,1)}) %all-gather.2.cloned.1.call-update) | async-done | bytes 16777232 | tf_op jit(solution)/shard_map/all_gather | solution.py:18
  901.4 368.7 %all_to_all.37 = bf16[2,2048,2048]{2,0,1:T(2,128)(2,1)S(1)} all-to-all(bf16[2,2048,2048]{2,0,1:T(2,128)(2,1)} %all-gather.2.cloned.1.call-done), channel_id=1, replica_groups=mesh['replica'=4,'fsdp'=8] {'fsdp'}, dimensions={1} | all-to-all | bytes 33554432 | tf_op jit(solution)/shard_map/all_to_all | solution.py:19
  1270.1 22.9 %copy.26 = bf16[2,256,8,2048]{3,2,1,0:T(8,128)(2,1)} copy(bf16[2,256,8,2048]{3,0,1,2:T(2,128)(2,1)S(1)} %bitcast.13) | data formatting | bytes 33554432 | tf_op jit(solution)/shard_map/all_to_all | solution.py:19
  1293.0 25.5 %all_to_all.33 = bf16[2,256,16384]{2,1,0:T(8,128)(2,1)} reshape(bf16[2,256,8,2048]{3,2,1,0:T(8,128)(2,1)} %copy.26) | data formatting | bytes 33554432 | tf_op jit(solution)/shard_map/all_to_all | solution.py:19
Async XLA Ops:
  7.2 760.7 %all-reduce.3.cloned.1.call-start = ((), (), s32[]{:S(2)}) async-start(), calls=%async_computation.3 | async-start | bytes 33554432
  480.3 0.7 copy-start
  480.3 421.1 %all-gather.2.cloned.1.call-start = ((), (), s32[]{:S(2)}) async-start(), calls=%async_computation.2 | async-start | bytes 20971520 | tf_op jit(solution)/shard_map/all_gather | solution.py:18
Sparse Core Ops, SparseCore 0:
  480.4 287.3 all-reduce.2
  795.5 105.9 all-gather.1
where the time goes:
time: 1330 us
  blocking collectives  741 us (56%)
  waiting for transfers between devices  392 us (29%)
  local copies, waits for them, and re-layouts  164 us (12%)
  between operations  14.7 us (1%)
  other arithmetic  13.9 us (1%)
    all_to_all x1, blocking collectives, on_device(): lax.all_to_all(local, 'fsdp', split_axis=2, concat_axis=1, tiled=True)  372 us
    all_to_all x1, blocking collectives, on_device(): lax.all_to_all(copies, 'fsdp', split_axis=1, concat_axis=2, tiled=True)  369 us
    unnamed x3, waiting for transfers between devices  286 us
    all_gather x1, waiting for transfers between devices, on_device(): copies = lax.all_gather(rounded, 'replica', axis=1, tiled=True)  106 us
    all_to_all x1, local copies, waits for them, and re-layouts, on_device(): lax.all_to_all(local, 'fsdp', split_axis=2, concat_axis=1, tiled=True)  60.3 us
    all_to_all x2, local copies, waits for them, and re-layouts, on_device(): lax.all_to_all(copies, 'fsdp', split_axis=1, concat_axis=2, tiled=True)  48.4 us
    unnamed x5, local copies, waits for them, and re-layouts  47 us
  transfers between devices with their start and end apart: 2, of which 2 were waited for; matrix products, arithmetic and copies ran while one was open for 0% of the time, Pallas kernels for 0%

commit v1 on v0

v1 whole, which is shorter than its diff:
```python
import functools

import jax
import jax.numpy as jnp
from jax import lax
from jax.experimental import pallas as pl
from jax.experimental.pallas import tpu as pltpu
from jax.sharding import PartitionSpec as P

F32, BF16 = jnp.float32, jnp.bfloat16
SPLITS = 4
AHEAD = 4
LAGS = (2, 5, 8, 10)


def kernel(
    dims, delta, master, momentum, master_out, momentum_out, out,
    own, half, cross, total, mas, mom,
    load, store, sent, pair_a, pair_b, cross_in, cross_side, total_in, back_in, side_in, last_in,
):
    R, F, PROJ, RB, FF, WD, H = dims
    B, X = F // R, R // PROJ
    RH, SUB, T = RB // X, WD // H, F * H
    w, f = lax.axis_index("replica"), lax.axis_index("fsdp")
    core, x = lax.rem(w, PROJ), w // PROJ
    a, b = f // B, lax.rem(f, B)
    other = 1 - core
    w_pair = x * PROJ + other
    w_side = (1 - x) * PROJ + core
    w_far = (1 - x) * PROJ + other
    pair, side = (w_pair, f), (w_side, f)
    near = x == a // PROJ
    far = jnp.logical_not(near)

    def turned(t):
        return lax.rem(t + t // F, 2) == 1

    def to(ref_src, ref_dst, send, recv, device):
        return pltpu.make_async_remote_copy(
            src_ref=ref_src, dst_ref=ref_dst, send_sem=send, recv_sem=recv,
            device_id=device, device_id_type=pl.DeviceIdType.MESH,
        )

    def block(worker, t):
        return lax.rem(lax.rem(t, F) + f + worker * B, F)

    def cols(worker, t):
        return pl.ds(pl.multiple_of(block(worker, t) * WD + (t // F) * SUB, 128), SUB)

    def rows(xi):
        return pl.ds(pl.multiple_of(xi * RH, RH), RH)

    def drain(ref, sem):
        pltpu.make_async_copy(ref, ref, sem).wait()

    barrier = pltpu.get_barrier_semaphore()
    mine = a == w

    def greet(device):
        pl.semaphore_signal(barrier, inc=1, device_id=device, device_id_type=pl.DeviceIdType.MESH)

    load_own = pltpu.make_async_copy(delta.at[core], own, load.at[0])
    load_mas = pltpu.make_async_copy(master, mas, load.at[1])
    load_mom = pltpu.make_async_copy(momentum, mom, load.at[2])
    load_own.start()
    load_mas.start()
    load_mom.start()
    greet(pair)
    greet(side)

    @pl.loop(0, F)
    def _(i):
        @pl.when(jnp.logical_not(jnp.logical_and(mine, i == f)))
        def _():
            greet((a, i))

        wi, bi = i // B, lax.rem(i, B)

        @pl.when(jnp.logical_not(jnp.logical_and(mine, jnp.logical_and(wi == w, bi == b))))
        def _():
            greet((wi, w * B + bi))

    @pl.when(mine)
    def _():
        pl.semaphore_wait(barrier, 2 * F)

    @pl.when(jnp.logical_not(mine))
    def _():
        pl.semaphore_wait(barrier, 2 * F + 2)

    def send_pair(t):
        cb, ca = cols(w_far, t), cols(w_pair, t)
        src = delta.at[other]
        to(src.at[rows(1 - x), cb], half.at[rows(1 - x), cb], sent.at[0], pair_b.at[t], pair).start()
        to(src.at[rows(x), ca], half.at[rows(x), ca], sent.at[0], pair_a.at[t], pair).start()

    def pair_sum(xi, c, arrived, send, recv):
        tile, mine_tile = half.at[rows(xi), c], own.at[rows(xi), c]
        pltpu.make_async_copy(tile, tile, arrived).wait()
        tile[...] = (tile[...].astype(F32) + mine_tile[...].astype(F32)).astype(BF16)
        to(tile, cross.at[rows(xi), c], send, recv, side).start()

    def step_cross(t):
        turn = turned(t)

        @pl.when(jnp.logical_not(jnp.logical_and(near, turn)))
        def _():
            pair_sum(1 - x, cols(w_side, t), pair_b.at[t], sent.at[1], cross_in.at[t])

        @pl.when(jnp.logical_and(far, turn))
        def _():
            pair_sum(x, cols(w, t), pair_a.at[t], sent.at[7], cross_side.at[t])

    def owner_slot(pi, bi, xi, t):
        return total.at[
            pi,
            pl.ds(pl.multiple_of(bi * RB + xi * RH, RH), RH),
            pl.ds(pl.multiple_of((t // F) * SUB, 128), SUB),
        ]

    def full_sum(worker, xi, t, arrived_pair, arrived_cross, send):
        c = cols(worker, t)
        tile, mine_tile, arrived = half.at[rows(xi), c], own.at[rows(xi), c], cross.at[rows(xi), c]
        pltpu.make_async_copy(tile, tile, arrived_pair).wait()
        pltpu.make_async_copy(arrived, arrived, arrived_cross).wait()
        tile[...] = (
            tile[...].astype(F32) + mine_tile[...].astype(F32) + arrived[...].astype(F32)
        ).astype(BF16)
        cb = block(worker, t)
        slot = owner_slot(core, b, xi, t)
        here = jnp.logical_and(mine, cb == f)

        @pl.when(here)
        def _():
            pltpu.make_async_copy(tile, slot, total_in.at[t]).start()

        @pl.when(jnp.logical_not(here))
        def _():
            to(tile, slot, send, total_in.at[t], (a, cb)).start()

    def step_total(t):
        turn = turned(t)

        @pl.when(jnp.logical_or(near, jnp.logical_not(turn)))
        def _():
            full_sum(w, x, t, pair_a.at[t], cross_in.at[t], sent.at[2])

        @pl.when(jnp.logical_and(near, turn))
        def _():
            full_sum(w_side, 1 - x, t, pair_b.at[t], cross_side.at[t], sent.at[6])

    def step_update(t):
        e = lax.rem(f + 2 * F - lax.rem(t, F) - w * B, F)
        we, be = e // B, lax.rem(e, B)
        pe, xe = lax.rem(we, PROJ), we // PROJ
        r0 = pl.multiple_of(be * RB + xe * RH, RH)
        rr = pl.ds(r0, RH)
        cc = pl.ds(pl.multiple_of((t // F) * SUB, 128), SUB)
        tile = owner_slot(pe, be, xe, t)
        pltpu.make_async_copy(tile, tile, total_in.at[t]).wait()
        m, v = mas.at[pe, rr, cc], mom.at[pe, rr, cc]
        outer = tile[...].astype(F32) / R
        velocity = 0.9 * v[...] + outer
        updated = m[...] - 0.7 * (outer + 0.9 * velocity)
        v[...] = velocity
        m[...] = updated
        tile[...] = updated.astype(BF16)
        pltpu.make_async_copy(m, master_out.at[pe, rr, cc], store.at[0]).start()
        pltpu.make_async_copy(v, momentum_out.at[pe, rr, cc], store.at[1]).start()
        fe = w * B + be
        dst = out.at[pe, rows(xe), pl.ds(pl.multiple_of(f * WD + (t // F) * SUB, 128), SUB)]
        here = jnp.logical_and(we == w, fe == f)

        @pl.when(here)
        def _():
            pltpu.make_async_copy(tile, dst, back_in.at[t]).start()

        @pl.when(jnp.logical_not(here))
        def _():
            to(tile, dst, sent.at[3], back_in.at[t], (we, fe)).start()

    def step_side(t):
        tile = out.at[core, rows(x), cols(w, t)]
        pltpu.make_async_copy(tile, tile, back_in.at[t]).wait()
        to(tile, tile, sent.at[4], side_in.at[t], side).start()
        to(tile, tile, sent.at[5], last_in, pair).start()

    def step_pair(t):
        tile = out.at[core, rows(1 - x), cols(w_side, t)]
        pltpu.make_async_copy(tile, tile, side_in.at[t]).wait()
        to(tile, tile, sent.at[5], last_in, pair).start()

    @pl.loop(0, min(AHEAD, T))
    def _(t):
        send_pair(t)

    load_own.wait()

    @pl.loop(0, T + LAGS[-1])
    def _(t):
        @pl.when(t + AHEAD < T)
        def _():
            send_pair(t + AHEAD)

        @pl.when(t < T)
        def _():
            step_cross(t)

        @pl.when(t == LAGS[1])
        def _():
            load_mas.wait()
            load_mom.wait()

        for lag, step in zip(LAGS, (step_total, step_update, step_side, step_pair)):
            @pl.when(jnp.logical_and(t >= lag, t < T + lag))
            def _():
                step(t - lag)

    drain(out.at[other], last_in)
    drain(half, sent.at[0])

    def drain_part(width, sem):
        drain(half.at[pl.ds(0, RH), pl.ds(0, width)], sem)

    @pl.when(mine)
    def _():
        drain_part(FF - WD, sent.at[2])
        drain_part((FF - WD) // 2, sent.at[6])
        drain_part(FF - WD, sent.at[3])

    @pl.when(jnp.logical_not(mine))
    def _():
        drain_part(FF, sent.at[3])

    @pl.when(jnp.logical_and(near, jnp.logical_not(mine)))
    def _():
        drain_part(FF, sent.at[2])
        drain_part(FF // 2, sent.at[6])

    @pl.when(near)
    def _():
        drain_part(FF // 2, sent.at[1])

    @pl.when(far)
    def _():
        drain_part(FF, sent.at[1])
        drain_part(FF // 2, sent.at[2])
        drain_part(FF // 2, sent.at[7])

    drain_part(FF, sent.at[4])
    drain(half, sent.at[5])
    drain(mas, store.at[0])
    drain(mom, store.at[1])


def on_device(deltas, master, momentum):
    local = deltas[0]
    R, F = lax.axis_size("replica"), lax.axis_size("fsdp")
    PROJ, RB, FF = local.shape
    WD = FF // F
    H = min(SPLITS, WD // 128)
    assert R == 2 * PROJ and PROJ == 2 and F % R == 0 and H % 2 == 0
    T = F * H
    hbm = pl.BlockSpec(memory_space=pl.ANY)
    dma = pltpu.SemaphoreType.DMA
    updated, velocity, params = pl.pallas_call(
        functools.partial(kernel, (R, F, PROJ, RB, FF, WD, H)),
        out_shape=(
            jax.ShapeDtypeStruct(master.shape, F32),
            jax.ShapeDtypeStruct(momentum.shape, F32),
            jax.ShapeDtypeStruct(local.shape, BF16),
        ),
        in_specs=[hbm] * 3,
        out_specs=(hbm,) * 3,
        scratch_shapes=[
            pltpu.VMEM((RB, FF), BF16),
            pltpu.VMEM((RB, FF), BF16),
            pltpu.VMEM((RB, FF), BF16),
            pltpu.VMEM(master.shape, BF16),
            pltpu.VMEM(master.shape, F32),
            pltpu.VMEM(master.shape, F32),
            dma((3,)), dma((2,)), dma((8,)),
            dma((T,)), dma((T,)), dma((T,)), dma((T,)), dma((T,)), dma((T,)), dma((T,)), dma,
        ],
        compiler_params=pltpu.CompilerParams(
            collective_id=0, has_side_effects=True, vmem_limit_bytes=56 * 2**20
        ),
    )(local, master, momentum)
    return updated, velocity, params


def solution(mesh):
    return jax.shard_map(
        on_device,
        mesh=mesh,
        in_specs=(
            P("replica", None, "fsdp", None),
            P(None, "replica", "fsdp"),
            P(None, "replica", "fsdp"),
        ),
        out_specs=(P(None, "replica", "fsdp"), P(None, "replica", "fsdp"), P(None, "fsdp", None)),
        check_vma=False,
    )
```

time: 1330 us -> 294 us (0.22)
  blocking collectives: 741 us -> 0 us
  waiting for transfers between devices: 392 us -> 0 us
  Pallas kernels: 0 us -> 269 us
  local copies, waits for them, and re-layouts: 164 us -> 23.1 us
  between operations: 14.7 us -> 0.68 us
  other arithmetic: 13.9 us -> 0.01 us
    all_to_all x2 -> x0, blocking collectives: 741 us -> none  [the longest x1 372 us: on_device(): lax.all_to_all(local, 'fsdp', split_axis=2, concat_axis=1, tiled=True)]
    unnamed x3 -> x0, waiting for transfers between devices: 286 us -> none
    pallas_call x0 -> x1, Pallas kernels: none -> 269 us  [on_device(): pl.pallas_call(functools.partial(kernel, (R, F, PROJ, RB, FF, WD, H)), ou...]
    all_to_all x3 -> x0, local copies, waits for them, and re-layouts: 109 us -> none  [the longest x1 60.3 us: on_device(): lax.all_to_all(local, 'fsdp', split_axis=2, concat_axis=1, tiled=True)]
    all_gather x1 -> x0, waiting for transfers between devices: 106 us -> none  [on_device(): copies = lax.all_gather(rounded, 'replica', axis=1, tiled=True)]
    unnamed x5 -> x11, local copies, waits for them, and re-layouts: 47 us -> 23.1 us
    convert_element_type x1 -> x0, other arithmetic: 13.9 us -> none  [on_device(): rounded = updated.astype(jnp.bfloat16)]
  transfers between devices with their start and end apart: 2 -> 0, of which waited for: 2 -> 0; matrix products, arithmetic and copies ran while one was open for 0% -> 0% of each run, Pallas kernels for 0% -> 0%
where the time goes in v1:
time: 294 us; the launch traced here: 293 us
  Pallas kernels  269 us (91%)
  local copies, waits for them, and re-layouts  23.1 us (8%)
    pallas_call x1, Pallas kernels, on_device(): pl.pallas_call(functools.partial(kernel, (R, F, PROJ, RB, FF, WD, H)), ou...  269 us
    unnamed x11, local copies, waits for them, and re-layouts  23.1 us

profile of v1, /device:TPU:0, one launch (start us, length us, event | category | flops | bytes accessed | tf_op | source)
XLA Modules:
  0.0 292.7 jit_solution(10104386146694173061)
XLA Ops:
  0.6 268.9 %shard_map.58 = (f32[2,512,2048]{2,1,0:T(8,128)}, f32[2,512,2048]{2,1,0:T(8,128)}, bf16[2,256,16384]{2,1,0:T(8,128)(2,1)}) custom-call(bf16[2,256,16384]{2,1,0:T(8,128)(2,1)} %bitcast.1, f32[2,512,2048]{2,1,0:T(8,128)} %master.1, f32[2,512,2048]{2,1,0:T(8,128)} %momentum.1), custom_call_target="tpu_custom_call" | custom-call | tf_op jit(solution)/shard_map/pallas_call | solution.py:266
  269.6 0.0 slice-start
  269.6 0.0 slice-start.1
  269.6 0.0 slice-start.2
  269.6 8.9 %copy.9 = f32[2,512,2048]{2,1,0:T(8,128)} copy(f32[2,512,2048]{2,1,0:T(8,128)} %get-tuple-element.6) | data formatting | bytes 16777216
  278.5 0.0 slice-start.3
  278.5 8.0 %copy.10 = f32[2,512,2048]{2,1,0:T(8,128)} copy(f32[2,512,2048]{2,1,0:T(8,128)} %get-tuple-element.7) | data formatting | bytes 16777216
  286.5 0.0 slice-done
  286.6 0.0 slice-done.1
  286.6 0.0 slice-done.2
  286.6 0.0 slice-done.3
  286.6 6.2 %copy.11 = bf16[2,256,16384]{2,1,0:T(8,128)(2,1)} copy(bf16[2,256,16384]{2,1,0:T(8,128)(2,1)S(1)} %bitcast.3) | data formatting | bytes 33554432
  (1 shorter events, 0.0 us)
Async XLA Ops:
  269.6 17.0 %slice-start = ((s8[16777216]{0:T(1024)(128)(4,1)}), s8[4194304]{0:T(1024)(128)(4,1)S(1)}, s32[]{:S(2)}) async-start(s8[16777216]{0:T(1024)(128)(4,1)} %bitcast.2), calls=%async_computation | async-start | bytes 8388608
  269.6 17.0 %slice-start.1 = ((s8[16777216]{0:T(1024)(128)(4,1)}), s8[4194304]{0:T(1024)(128)(4,1)S(1)}, s32[]{:S(2)}) async-start(s8[16777216]{0:T(1024)(128)(4,1)} %bitcast.2), calls=%async_computation.1 | async-start | bytes 8388608
  269.6 17.0 %slice-start.2 = ((s8[16777216]{0:T(1024)(128)(4,1)}), s8[4194304]{0:T(1024)(128)(4,1)S(1)}, s32[]{:S(2)}) async-start(s8[16777216]{0:T(1024)(128)(4,1)} %bitcast.2), calls=%async_computation.2 | async-start | bytes 8388608
  278.5 8.1 %slice-start.3 = ((s8[16777216]{0:T(1024)(128)(4,1)}), s8[4194304]{0:T(1024)(128)(4,1)S(1)}, s32[]{:S(2)}) async-start(s8[16777216]{0:T(1024)(128)(4,1)} %bitcast.2), calls=%async_computation.3 | async-start | bytes 8388608
